TPU v7x, 32 devices: a whole 2x2x4 slice. The times are simulated.
32 devices in a mesh: grp: 2 (over x), leaf: 16 (over z, y, core).
Axes of the slice: x: 2, y: 2, z: 4, core: 2. Of those that a mesh axis runs over, the one named last changes fastest.
Arguments:
- points: float32 [8, 32768], P(None, ('grp', 'leaf')), may hold values from -6 to 6
- rhs: float32 [16, 32768], P(None, ('grp', 'leaf')), may hold values from -6 to 6
- basis: float32 [32768, 128], P(('grp', 'leaf')), may hold values from -0.1875 to 0.1875
- transfer: float32 [32, 128, 128], P(('grp', 'leaf')), may hold values from -0.5 to 0.5
- noise: float32 [32768], P(('grp', 'leaf')), may hold values from 0.5 to 2
- inv_scale: float32 [8], replicated, may hold values from 0.15 to 0.6
- links: int32 [32, 2], P(('grp', 'leaf')), may hold values from 0 to 1, as said below
- leaf_skel: int32 [32, 128], P(('grp', 'leaf')), may hold values from 0 to 1023, as said below
- group_skel: int32 [2, 128], P('grp'), may hold values from 0 to 2047, as said below
Outputs:
- solution: float32 [16, 32768], P(None, ('grp', 'leaf'))
- residual: float32 [16, 32768], P(None, ('grp', 'leaf'))
Inputs may be any that keep to these rules, and one draw needn't show every extreme that they name: `links`: column 1 of box l equals column 0 of box l + 1; column 0 is 0 for the first box of each group of 16 and column 1 for the last. `leaf_skel`: the 128 indices of a box are distinct. `group_skel`: the 128 indices of a group are distinct.
All inputs are finite; a program needn't handle non-finite values.
Results may differ from a plain program's by a relative error of at most 0.0003.
Values sent between devices are 32-bit elements; how exact they have to be, the bound alone decides.
No kernel may reach another device: no remote copies, remote signals or barrier semaphores. Data moves between devices by JAX's collectives and lax.ppermute only.
A program may use at most 128 MiB of HBM per device.

v0:
```python
import jax
import jax.numpy as jnp
from jax import lax
from jax.sharding import PartitionSpec as P

ITERS = 2


def padded_2(value, sides, width):
    for axis, dim in sides:
        size, length = (lax.axis_size(axis), value.shape[dim])
        up = [(i, (i + 1) % size) for i in range(size - 1)]
        down = [(j, i) for i, j in up]
        last = lax.slice_in_dim(value, length - width, length, axis=dim)
        initial = lax.slice_in_dim(value, 0, width, axis=dim)
        before = lax.ppermute(last, axis, up)
        after = lax.ppermute(initial, axis, down)
        value = jnp.concatenate([before, value, after], axis=dim)
    return value


def kernel_block(left, right, inv_scale):
    first = left * inv_scale[:, None]
    second = right * inv_scale[:, None]
    cross = lax.dot_general(
        first, second, (((0,), (0,)), ((), ())), precision=lax.Precision.HIGHEST
    )
    dist = (
        jnp.sum(first * first, axis=0)[:, None]
        + jnp.sum(second * second, axis=0)[None, :]
        - 2.0 * cross
    )
    scaled = jnp.sqrt(5.0 * jnp.maximum(dist, 0.0))
    return (1.0 + scaled + scaled * scaled / 3.0) * jnp.exp(-scaled)


def contract(first, second):
    return lax.dot_general(first, second, (((1,), (1,)), ((), ())), precision=lax.Precision.HIGHEST)


def product(first, second):
    return jnp.dot(first, second, precision=lax.Precision.HIGHEST)


def two_products(residual, image):
    return lax.psum(
        (jnp.sum(residual * residual, axis=1), jnp.sum(residual * image, axis=1)), ("grp", "leaf")
    )


def local(points, rhs, basis, transfer, noise, inv_scale, links, leaf_skel, group_skel):
    width = points.shape[1]
    left_bit = links[0, 0]
    right_bit = links[0, 1]
    weight_self = 1.0 + (left_bit + right_bit).astype(jnp.float32)
    skel_pts = points[:, leaf_skel[0]]
    group_pts = lax.all_gather(skel_pts, "leaf", axis=1, tiled=True)
    top_pts = group_pts[:, group_skel[0]]
    top_all = lax.all_gather(top_pts, "grp", axis=1, tiled=True)
    kernel_top = kernel_block(top_pts, top_all, inv_scale)
    kernel_far = kernel_block(skel_pts, group_pts, inv_scale)
    kernel_self = kernel_block(points, points, inv_scale)
    square_zero = jnp.zeros((width, width), jnp.float32)
    lift = transfer[0]
    beside_all = padded_2(points, (("leaf", 1),), width)
    kernel_left = lax.cond(
        left_bit > 0,
        lambda: kernel_block(beside_all[:, :width], points, inv_scale),
        lambda: square_zero,
    )
    kernel_right = lax.cond(
        right_bit > 0,
        lambda: kernel_block(beside_all[:, 2 * width :], points, inv_scale),
        lambda: square_zero,
    )

    def near_part(vec):
        padded = padded_2(vec, (("leaf", 1),), width)
        result = weight_self * product(vec, kernel_self)
        result = result + product(padded[:, :width], kernel_left)
        return result + product(padded[:, 2 * width :], kernel_right)

    def apply(vec):
        coeff = product(vec, basis)
        far = contract(lax.all_gather(coeff, "leaf", axis=1, tiled=True), kernel_far)
        group_coeff = lax.psum(product(coeff, lift), "leaf")
        top_coeff = lax.all_gather(group_coeff, "grp", axis=1, tiled=True)
        top = contract(top_coeff, kernel_top)
        row = far + contract(top, lift)
        return noise[None, :] * vec + near_part(vec) + contract(row, basis)

    solution = jnp.zeros_like(rhs)
    residual = rhs
    image = apply(residual)
    norm_now, curve = two_products(residual, image)
    alpha = norm_now / curve
    direction, along = (residual, image)
    for step in range(ITERS):
        solution = solution + alpha[:, None] * direction
        residual = residual - alpha[:, None] * along
        if step + 1 < ITERS:
            image = apply(residual)
            norm_next, curve = two_products(residual, image)
            ratio = norm_next / norm_now
            alpha = norm_next / (curve - ratio * norm_next / alpha)
            direction = residual + ratio[:, None] * direction
            along = image + ratio[:, None] * along
            norm_now = norm_next
    return (solution, residual)


def solution(mesh):
    return jax.shard_map(
        local,
        mesh=mesh,
        in_specs=(
            P(None, ("grp", "leaf")),
            P(None, ("grp", "leaf")),
            P(("grp", "leaf"), None),
            P(("grp", "leaf"), None, None),
            P(("grp", "leaf")),
            P(),
            P(("grp", "leaf"), None),
            P(("grp", "leaf"), None),
            P("grp", None),
        ),
        out_specs=(P(None, ("grp", "leaf")), P(None, ("grp", "leaf"))),
        check_vma=False,
    )
```

profile of v0, /device:TPU:10, one launch (start us, length us, event | category | flops | bytes accessed | tf_op | source)
XLA Modules:
  0.0 289.5 jit_solution(12969170760022450725)
XLA Ops:
  0.6 0.0 copy-start
  0.6 2.9 collective-permute-start.2
  3.5 1.9 collective-permute-start
  5.5 4.5 %collective-permute-start.3 = (f32[16,1024]{1,0:T(8,128)}, f32[16,1024]{1,0:T(8,128)S(1)}, u32[]{:S(2)}, u32[]{:S(2)}) collective-permute-start(f32[16,1024]{1,0:T(8,128)} %param.14), channel_id=1, source_target_pairs={{1,0},{2,1},{3,2},{4,3},{5,4},{6,5},{7,6},{8,7},{9,8},{10,9},{11,1... | collective-permute-start | bytes 196616 | tf_op jit(solution)/shard_map/ppermute | solution.py:17
  10.0 1.9 collective-permute-start.1
  12.0 1.0 copy.11
  12.9 0.7 fusion.35
  13.6 0.7 fusion.36
  14.2 1.3 fusion.39
  16.9 0.8 multiply_reduce_fusion.12
  17.7 1.2 fusion.41
  18.9 17.5 %all_gather.18 = f32[16,2048]{1,0:T(8,128)S(1)} all-gather(f32[16,128]{1,0:T(8,128)S(1)} %fusion.41), channel_id=1, replica_groups=mesh['grp'=2,'leaf'=16] {'leaf'}, dimensions={1}, use_global_device_ids=true | all-gather | bytes 139264 | tf_op jit(solution)/shard_map/all_gather | solution.py:85
  36.4 1.0 fusion.26
  37.4 25.1 %psum.43 = f32[16,128]{1,0:T(8,128)S(1)} all-reduce(f32[16,128]{1,0:T(8,128)S(1)} %fusion.26), channel_id=1, replica_groups=mesh['grp'=2,'leaf'=16] {'leaf'}, use_global_device_ids=true, to_apply=%region_13.14 | all-reduce | flops 2048 | bytes 16384 | tf_op jit(solution)/shard_map/psum | solution.py:86
  62.5 4.4 %all_gather.20 = f32[16,256]{1,0:T(8,128)S(1)} all-gather(f32[16,128]{1,0:T(8,128)S(1)} %psum.43), channel_id=1, replica_groups=mesh['grp'=2,'leaf'=16] {'grp'}, dimensions={1}, use_global_device_ids=true | all-gather | bytes 24576 | tf_op jit(solution)/shard_map/all_gather | solution.py:87
  66.8 0.6 gather_fusion
  67.5 25.8 %all-gather = f32[8,2048]{0,1:T(8,128)S(1)} all-gather(f32[8,128]{0,1:T(8,128)S(1)} %bitcast.71), channel_id=2, replica_groups=mesh['grp'=2,'leaf'=16] {'leaf'}, dimensions={1}, use_global_device_ids=true | all-gather | bytes 69632 | tf_op jit(solution)/shard_map/all_gather | solution.py:57
  93.2 1.0 multiply_reduce_fusion.4
  94.2 0.6 gather_fusion.1
  94.9 0.8 multiply_reduce_fusion.9
  95.7 5.0 %all-gather.1 = f32[8,256]{0,1:T(8,128)S(1)} all-gather(f32[8,128]{0,1:T(8,128)S(1)} %bitcast.70), channel_id=3, replica_groups=mesh['grp'=2,'leaf'=16] {'grp'}, dimensions={1}, use_global_device_ids=true | all-gather | bytes 12288 | tf_op jit(solution)/shard_map/all_gather | solution.py:59
  100.7 0.8 multiply_reduce_fusion.5
  101.5 0.0 copy-start.8
  101.5 6.9 %exponential_multiply_fusion.2 = f32[1024,1024]{1,0:T(8,128)S(1)} fusion(f32[1024]{0:T(1024)S(1)} %multiply_reduce_fusion.12, f32[8,1024]{1,0:T(8,128)} %param.13, f32[8]{0:T(128)} %param.18), kind=kOutput, calls=%fused_computation.14 | convolution fusion | flops 112205824 | bytes 4231200 | tf_op jit(solution)/shard_map/dot_general | solution.py:25
  108.3 0.0 copy-start.5
  108.4 0.0 copy-start.4
  108.4 1.6 exponential_multiply_fusion.3
  110.0 0.0 copy-start.6
  110.0 0.9 fusion.42
  110.9 0.4 exponential_multiply_fusion.4
  111.3 0.2 fusion.43
  111.5 0.0 copy-done.5
  111.5 0.2 convolution_add_fusion.3
  111.7 0.0 copy-done.4
  111.7 2.3 convolution_multiply_fusion.3
  114.1 0.0 copy-done.3
  114.1 0.5 fusion.44
  115.9 0.0 collective-permute-done
  115.9 2.5 conditional.2
  115.9 2.5 broadcast.88
  118.4 2.5 conditional.3
  118.4 2.5 broadcast.94
  120.9 4.6 %fusion.40 = f32[1024,16]{0,1:T(8,128)S(1)} fusion(f32[1024,1024]{1,0:T(8,128)} %get-tuple-element.49, f32[16,1024]{1,0:T(8,128)S(1)} %collective-permute-done.3), kind=kOutput, calls=%fused_computation.77 | convolution fusion | flops 201326592 | bytes 4325376 | tf_op jit(solution)/shard_map/dot_general | solution.py:42
  125.5 0.0 collective-permute-done.1
  125.6 2.4 multiply_reduce_fusion.8
  128.0 49.4 %all-reduce.1 = (f32[16]{0:T(128)S(1)}, f32[16]{0:T(128)S(1)}) all-reduce(f32[16]{0:T(128)S(1)} %get-tuple-element.33, f32[16]{0:T(128)S(1)} %get-tuple-element.32), channel_id=1, replica_groups=mesh['grp'=2,'leaf'=16] {'grp','leaf'}, use_global_device_ids=true, to_apply=%region_1.0 | all-reduce | flops 32 | bytes 256 | tf_op jit(solution)/shard_map/psum | solution.py:46
  177.4 0.1 multiply_subtract_fusion.1
  177.4 4.3 %convolution_multiply_fusion.2 = f32[16,1024]{1,0:T(8,128)S(1)} fusion(f32[16,1024]{1,0:T(8,128)S(1)} %multiply_subtract_fusion.1, f32[1024,1024]{1,0:T(8,128)} %copy-done.3, f32[]{:T(128)} %bitcast), kind=kOutput, calls=%fused_computation.26 | convolution fusion | flops 201342976 | bytes 4325380 | tf_op jit(solution)/shard_map/dot_general | solution.py:42
  181.7 0.4 fusion.46
  182.1 1.9 collective-permute-start.5
  184.0 2.4 collective-permute-start.4
  186.4 0.2 fusion.23
  186.6 16.7 %all_gather.22 = f32[16,2048]{1,0:T(8,128)S(1)} all-gather(f32[16,128]{1,0:T(8,128)S(1)} %fusion.46), channel_id=1, replica_groups=mesh['grp'=2,'leaf'=16] {'leaf'}, dimensions={1}, use_global_device_ids=true | all-gather | bytes 139264 | tf_op jit(solution)/shard_map/all_gather | solution.py:85
  203.3 25.0 %psum.46 = f32[16,128]{1,0:T(8,128)S(1)} all-reduce(f32[16,128]{1,0:T(8,128)S(1)} %fusion.23), channel_id=1, replica_groups=mesh['grp'=2,'leaf'=16] {'leaf'}, use_global_device_ids=true, to_apply=%region_20.0 | all-reduce | flops 2048 | bytes 16384 | tf_op jit(solution)/shard_map/psum | solution.py:86
  228.3 4.5 %all_gather.23 = f32[16,256]{1,0:T(8,128)S(1)} all-gather(f32[16,128]{1,0:T(8,128)S(1)} %psum.46), channel_id=1, replica_groups=mesh['grp'=2,'leaf'=16] {'grp'}, dimensions={1}, use_global_device_ids=true | all-gather | bytes 24576 | tf_op jit(solution)/shard_map/all_gather | solution.py:87
  232.8 0.2 fusion.48
  233.0 1.0 fusion.47
  234.0 0.2 convolution_add_fusion.2
  234.1 0.0 collective-permute-done.5
  234.2 4.3 %fusion.45 = f32[16,1024]{1,0:T(8,128)S(1)} fusion(f32[16,1024]{1,0:T(8,128)S(1)} %collective-permute-done.5, f32[1024,1024]{1,0:T(8,128)} %get-tuple-element.49), kind=kOutput, calls=%fused_computation.82 | convolution fusion | flops 201326592 | bytes 4325376 | tf_op jit(solution)/shard_map/dot_general | solution.py:42
  238.5 2.1 fusion.18
  240.6 0.6 multiply_reduce_fusion.6
  241.2 47.5 %all-reduce = (f32[16]{0:T(128)S(1)}, f32[16]{0:T(128)S(1)}) all-reduce(f32[16]{0:T(128)S(1)} %get-tuple-element.31, f32[16]{0:T(128)S(1)} %get-tuple-element.30), channel_id=1, replica_groups=mesh['grp'=2,'leaf'=16] {'grp','leaf'}, use_global_device_ids=true, to_apply=%region_19.0 | all-reduce | flops 32 | bytes 256 | tf_op jit(solution)/shard_map/psum | solution.py:46
  288.8 0.7 multiply_subtract_fusion
  (17 shorter events, 0.1 us)
Async XLA Ops:
  0.6 17.1 %copy-start = (f32[1024,128]{1,0:T(8,128)S(1)}, f32[1024,128]{1,0:T(8,128)}, u32[]{:S(2)}) copy-start(f32[1024,128]{1,0:T(8,128)} %param.15) | copy-start | bytes 1572868
  0.6 117.8 %collective-permute-start.2 = (f32[8,1024]{1,0:T(8,128)}, f32[8,1024]{1,0:T(8,128)S(1)}, u32[]{:S(2)}, u32[]{:S(2)}) collective-permute-start(f32[8,1024]{1,0:T(8,128)} %param.13), channel_id=1, source_target_pairs={{1,0},{2,1},{3,2},{4,3},{5,4},{6,5},{7,6},{8,7},{9,8},{10,9},{11,1... | collective-permute-start | bytes 98312 | tf_op jit(solution)/shard_map/ppermute | solution.py:17
  3.5 112.4 %collective-permute-start = (f32[8,1024]{1,0:T(8,128)}, f32[8,1024]{1,0:T(8,128)S(1)}, u32[]{:S(2)}, u32[]{:S(2)}) collective-permute-start(f32[8,1024]{1,0:T(8,128)} %param.13), channel_id=1, source_target_pairs={{0,1},{1,2},{2,3},{3,4},{4,5},{5,6},{6,7},{7,8},{8,9},{9,10},{10,1... | collective-permute-start | bytes 98312 | tf_op jit(solution)/shard_map/ppermute | solution.py:16
  5.5 115.5 %collective-permute-start.3 = (f32[16,1024]{1,0:T(8,128)}, f32[16,1024]{1,0:T(8,128)S(1)}, u32[]{:S(2)}, u32[]{:S(2)}) collective-permute-start(f32[16,1024]{1,0:T(8,128)} %param.14), channel_id=1, source_target_pairs={{1,0},{2,1},{3,2},{4,3},{5,4},{6,5},{7,6},{8,7},{9,8},{10,9},{11,1... | collective-permute-start | bytes 196616 | tf_op jit(solution)/shard_map/ppermute | solution.py:17
  10.0 115.5 %collective-permute-start.1 = (f32[16,1024]{1,0:T(8,128)}, f32[16,1024]{1,0:T(8,128)S(1)}, u32[]{:S(2)}, u32[]{:S(2)}) collective-permute-start(f32[16,1024]{1,0:T(8,128)} %param.14), channel_id=1, source_target_pairs={{0,1},{1,2},{2,3},{3,4},{4,5},{5,6},{6,7},{7,8},{8,9},{9,10},{10,1... | collective-permute-start | bytes 196616 | tf_op jit(solution)/shard_map/ppermute | solution.py:16
  101.5 6.9 %copy-start.8 = (f32[8]{0:T(128)S(1)}, f32[8]{0:T(128)}, u32[]{:S(2)}) copy-start(f32[8]{0:T(128)} %param.18) | copy-start | bytes 100
  108.3 5.7 %copy-start.3 = (f32[1024,1024]{1,0:T(8,128)}, f32[1024,1024]{1,0:T(8,128)S(1)}, u32[]{:S(2)}) copy-start(f32[1024,1024]{1,0:T(8,128)S(1)} %exponential_multiply_fusion.2) | copy-start | bytes 12582916
  108.3 3.1 %copy-start.5 = (f32[1,128,128]{2,1,0:T(8,128)S(1)}, f32[1,128,128]{2,1,0:T(8,128)}, u32[]{:S(2)}) copy-start(f32[1,128,128]{2,1,0:T(8,128)} %param.16) | copy-start | bytes 196612
  108.4 3.4 %copy-start.4 = (f32[16,1024]{1,0:T(8,128)S(1)}, f32[16,1024]{1,0:T(8,128)}, u32[]{:S(2)}) copy-start(f32[16,1024]{1,0:T(8,128)} %param.14) | copy-start | bytes 196612
  110.0 5.9 %copy-start.6 = (f32[8,1024]{1,0:T(8,128)S(1)}, f32[8,1024]{1,0:T(8,128)}, u32[]{:S(2)}) copy-start(f32[8,1024]{1,0:T(8,128)} %param.13) | copy-start | bytes 98308
  120.9 4.6 %copy-start.7 = (f32[1024]{0:T(1024)S(1)}, f32[1024]{0:T(1024)}, u32[]{:S(2)}) copy-start(f32[1024]{0:T(1024)} %param.17) | copy-start | bytes 12292
  120.9 4.6 %copy-start.1 = (f32[1024,1024]{1,0:T(8,128)S(1)}, f32[1024,1024]{1,0:T(8,128)}, u32[]{:S(2)}) copy-start(f32[1024,1024]{1,0:T(8,128)} %get-tuple-element.48) | copy-start | bytes 12582916
  182.1 52.1 %collective-permute-start.5 = (f32[16,1024]{1,0:T(8,128)S(1)}, f32[16,1024]{1,0:T(8,128)S(1)}, u32[]{:S(2)}, u32[]{:S(2)}) collective-permute-start(f32[16,1024]{1,0:T(8,128)S(1)} %multiply_subtract_fusion.1), channel_id=1, source_target_pairs={{1,0},{2,1},{3,2},{4,3},{5,4},{6,5},{7,6},{8,7},{9,8},{10,9},{11,1... | collective-permute-start | bytes 196616 | tf_op jit(solution)/shard_map/ppermute | solution.py:17
  184.0 54.5 %collective-permute-start.4 = (f32[16,1024]{1,0:T(8,128)S(1)}, f32[16,1024]{1,0:T(8,128)S(1)}, u32[]{:S(2)}, u32[]{:S(2)}) collective-permute-start(f32[16,1024]{1,0:T(8,128)S(1)} %multiply_subtract_fusion.1), channel_id=1, source_target_pairs={{0,1},{1,2},{2,3},{3,4},{4,5},{5,6},{6,7},{7,8},{8,9},{9,10},{10,1... | collective-permute-start | bytes 196616 | tf_op jit(solution)/shard_map/ppermute | solution.py:16
  228.3 10.2 %copy-start.2 = (f32[1024,1024]{1,0:T(8,128)S(1)}, f32[1024,1024]{1,0:T(8,128)}, u32[]{:S(2)}) copy-start(f32[1024,1024]{1,0:T(8,128)} %get-tuple-element.48) | copy-start | bytes 12582916
where the time goes:
time: 290 us
  blocking collectives  221 us (76%)
  matrix products  35.3 us (12%)
  starting transfers between devices  15.6 us (5%)
  local copies, waits for them, and re-layouts  8.64 us (3%)
  other arithmetic  5.55 us (2%)
  between operations  3.6 us (1%)
    psum x2, blocking collectives, two_products(): lax.psum((jnp.sum(residual * residual, axis=1), jnp.sum(residual * image,...  96.9 us
    psum x2, blocking collectives, apply(): group_coeff = lax.psum(product(coeff, lift), 'leaf')  50.1 us
    all_gather x2, blocking collectives, apply(): lax.all_gather(coeff, 'leaf', axis=1, tiled=True)  34.1 us
    all_gather x1, blocking collectives, local(): group_pts = lax.all_gather(skel_pts, 'leaf', axis=1, tiled=True)  25.8 us
    dot_general x10, matrix products, product(): return jnp.dot(first, second, precision=lax.Precision.HIGHEST)  22.7 us
    ppermute x3, starting transfers between devices, padded_2(): after = lax.ppermute(initial, axis, down)  9.35 us
    all_gather x2, blocking collectives, apply(): top_coeff = lax.all_gather(group_coeff, 'grp', axis=1, tiled=True)  8.85 us
    dot_general x3, matrix products, kernel_block(): lax.dot_general(first, second, (((0,), (0,)), ((), ())), precision=lax.Pr...  8.84 us
  transfers between devices with their start and end apart: 6, of which 0 were waited for; matrix products, arithmetic and copies ran while one was open for 13% of the time, Pallas kernels for 0%

commit v1 on v0

--- a/solution.py
+++ b/solution.py
@@ -83,7 +83,7 @@
     def apply(vec):
         coeff = product(vec, basis)
         far = contract(lax.all_gather(coeff, "leaf", axis=1, tiled=True), kernel_far)
-        group_coeff = lax.psum(product(coeff, lift), "leaf")
+        group_coeff = lax.all_gather(product(coeff, lift), "leaf").sum(axis=0)
         top_coeff = lax.all_gather(group_coeff, "grp", axis=1, tiled=True)
         top = contract(top_coeff, kernel_top)
         row = far + contract(top, lift)

time: 290 us -> 267 us (0.921)
  blocking collectives: 221 us -> 199 us
    psum x2 -> x0, blocking collectives: 50.1 us -> none  [apply(): group_coeff = lax.psum(product(coeff, lift), 'leaf')]
    all_gather x0 -> x2, blocking collectives: none -> 35.6 us  [apply(): group_coeff = lax.all_gather(product(coeff, lift), 'leaf').sum(axis=0)]
    psum x2, blocking collectives: 96.9 us -> 92.8 us  [two_products(): lax.psum((jnp.sum(residual * residual, axis=1), jnp.sum(residual * image,...]
    all_gather x1, blocking collectives: 25.8 us -> 21.8 us  [local(): group_pts = lax.all_gather(skel_pts, 'leaf', axis=1, tiled=True)]
  transfers between devices with their start and end apart: 6 -> 6, of which waited for: 0 -> 0; matrix products, arithmetic and copies ran while one was open for 13% -> 14% of each run, Pallas kernels for 0% -> 0%
where the time goes in v1:
time: 267 us; the launch traced here: 266 us
  blocking collectives  199 us (75%)
  matrix products  34.4 us (13%)
  starting transfers between devices  15.6 us (6%)
  local copies, waits for them, and re-layouts  8.64 us (3%)
  other arithmetic  4.93 us (2%)
  between operations  3.58 us (1%)
    psum x2, blocking collectives, two_products(): lax.psum((jnp.sum(residual * residual, axis=1), jnp.sum(residual * image,...  92.8 us
    all_gather x2, blocking collectives, apply(): group_coeff = lax.all_gather(product(coeff, lift), 'leaf').sum(axis=0)  35.6 us
    all_gather x2, blocking collectives, apply(): lax.all_gather(coeff, 'leaf', axis=1, tiled=True)  34.6 us
    dot_general x10, matrix products, product(): return jnp.dot(first, second, precision=lax.Precision.HIGHEST)  22.7 us
    all_gather x1, blocking collectives, local(): group_pts = lax.all_gather(skel_pts, 'leaf', axis=1, tiled=True)  21.8 us
    ppermute x3, starting transfers between devices, padded_2(): after = lax.ppermute(initial, axis, down)  9.35 us
    all_gather x2, blocking collectives, apply(): top_coeff = lax.all_gather(group_coeff, 'grp', axis=1, tiled=True)  8.85 us
    dot_general x3, matrix products, kernel_block(): lax.dot_general(first, second, (((0,), (0,)), ((), ())), precision=lax.Pr...  8 us
  transfers between devices with their start and end apart: 6, of which 0 were waited for; matrix products, arithmetic and copies ran while one was open for 14% of the time, Pallas kernels for 0%

profile of v1, /device:TPU:10, one launch (start us, length us, event | category | flops | bytes accessed | tf_op | source)
XLA Modules:
  0.0 265.9 jit_solution(65771734738916759)
XLA Ops:
  0.6 0.0 copy-start
  0.6 0.0 copy-start.6
  0.7 0.0 copy-start.8
  0.7 2.9 %collective-permute-start.2 = (f32[8,1024]{1,0:T(8,128)}, f32[8,1024]{1,0:T(8,128)S(1)}, u32[]{:S(2)}, u32[]{:S(2)}) collective-permute-start(f32[8,1024]{1,0:T(8,128)} %param.13), channel_id=1, source_target_pairs={{1,0},{2,1},{3,2},{4,3},{5,4},{6,5},{7,6},{8,7},{9,8},{10,9},{11,1... | collective-permute-start | bytes 98312 | tf_op jit(solution)/shard_map/ppermute | solution.py:17
  3.6 1.9 collective-permute-start
  5.5 4.5 %collective-permute-start.3 = (f32[16,1024]{1,0:T(8,128)}, f32[16,1024]{1,0:T(8,128)S(1)}, u32[]{:S(2)}, u32[]{:S(2)}) collective-permute-start(f32[16,1024]{1,0:T(8,128)} %param.14), channel_id=1, source_target_pairs={{1,0},{2,1},{3,2},{4,3},{5,4},{6,5},{7,6},{8,7},{9,8},{10,9},{11,1... | collective-permute-start | bytes 196616 | tf_op jit(solution)/shard_map/ppermute | solution.py:17
  10.0 1.9 collective-permute-start.1
  12.0 1.0 copy.11
  12.9 0.7 fusion.35
  13.6 0.7 fusion.36
  14.3 1.3 fusion.39
  16.9 0.8 multiply_reduce_fusion.12
  17.8 1.2 fusion.41
  19.0 17.5 %all_gather.30 = f32[16,2048]{1,0:T(8,128)S(1)} all-gather(f32[16,128]{1,0:T(8,128)S(1)} %fusion.41), channel_id=1, replica_groups=mesh['grp'=2,'leaf'=16] {'leaf'}, dimensions={1}, use_global_device_ids=true | all-gather | bytes 139264 | tf_op jit(solution)/shard_map/all_gather | solution.py:85
  36.4 1.0 fusion.26
  37.4 17.8 %all-gather.1 = f32[256,128]{1,0:T(8,128)S(1)} all-gather(f32[16,128]{1,0:T(8,128)S(1)} %fusion.26), channel_id=3, replica_groups=mesh['grp'=2,'leaf'=16] {'leaf'}, dimensions={0}, use_global_device_ids=true | all-gather | bytes 139264 | tf_op jit(solution)/shard_map/all_gather | solution.py:86
  55.2 4.4 %all_gather.34 = f32[16,256]{1,0:T(8,128)S(1)} all-gather(f32[16,128]{1,0:T(8,128)S(1)} %reduce_sum.143), channel_id=1, replica_groups=mesh['grp'=2,'leaf'=16] {'grp'}, dimensions={1}, use_global_device_ids=true | all-gather | bytes 24576 | tf_op jit(solution)/shard_map/all_gather | solution.py:87
  59.6 0.6 gather_fusion
  60.2 21.8 %all-gather = f32[8,2048]{0,1:T(8,128)S(1)} all-gather(f32[8,128]{0,1:T(8,128)S(1)} %bitcast.75), channel_id=2, replica_groups=mesh['grp'=2,'leaf'=16] {'leaf'}, dimensions={1}, use_global_device_ids=true | all-gather | bytes 69632 | tf_op jit(solution)/shard_map/all_gather | solution.py:57
  82.1 1.0 multiply_reduce_fusion.4
  83.1 0.6 gather_fusion.1
  83.7 0.8 multiply_reduce_fusion.9
  84.5 5.0 %all-gather.2 = f32[8,256]{0,1:T(8,128)S(1)} all-gather(f32[8,128]{0,1:T(8,128)S(1)} %bitcast.74), channel_id=4, replica_groups=mesh['grp'=2,'leaf'=16] {'grp'}, dimensions={1}, use_global_device_ids=true | all-gather | bytes 12288 | tf_op jit(solution)/shard_map/all_gather | solution.py:59
  89.5 0.1 multiply_reduce_fusion.5
  89.6 6.0 %exponential_multiply_fusion.2 = f32[1024,1024]{1,0:T(8,128)S(1)} fusion(f32[1024]{0:T(1024)S(1)} %multiply_reduce_fusion.12, f32[8,1024]{1,0:T(8,128)S(1)} %copy-done.6, f32[8]{0:T(128)S(1)} %copy-done.8), kind=kOutput, calls=%fused_computation.14 | convolution fusion | flops 112205824 | bytes 4231200 | tf_op jit(solution)/shard_map/dot_general | solution.py:25
  95.7 0.0 copy-start.5
  95.7 0.0 copy-start.4
  95.7 1.6 exponential_multiply_fusion.3
  97.3 0.9 fusion.42
  98.2 0.4 exponential_multiply_fusion.4
  98.6 0.2 fusion.43
  98.8 0.0 copy-done.5
  98.8 0.2 convolution_add_fusion.3
  99.0 0.0 copy-done.4
  99.1 2.3 convolution_multiply_fusion.3
  101.4 0.0 copy-done.3
  101.4 0.5 fusion.44
  103.2 0.0 collective-permute-done
  103.2 2.5 conditional.2
  103.2 2.5 broadcast.88
  105.7 2.5 conditional.3
  105.7 2.5 broadcast.94
  108.2 4.6 %fusion.40 = f32[1024,16]{0,1:T(8,128)S(1)} fusion(f32[1024,1024]{1,0:T(8,128)} %get-tuple-element.49, f32[16,1024]{1,0:T(8,128)S(1)} %collective-permute-done.3), kind=kOutput, calls=%fused_computation.77 | convolution fusion | flops 201326592 | bytes 4325376 | tf_op jit(solution)/shard_map/dot_general | solution.py:42
  112.8 0.0 collective-permute-done.1
  112.9 2.4 multiply_reduce_fusion.8
  115.3 49.8 %all-reduce.1 = (f32[16]{0:T(128)S(1)}, f32[16]{0:T(128)S(1)}) all-reduce(f32[16]{0:T(128)S(1)} %get-tuple-element.33, f32[16]{0:T(128)S(1)} %get-tuple-element.32), channel_id=1, replica_groups=mesh['grp'=2,'leaf'=16] {'grp','leaf'}, use_global_device_ids=true, to_apply=%region_1.0 | all-reduce | flops 32 | bytes 256 | tf_op jit(solution)/shard_map/psum | solution.py:46
  165.1 0.1 multiply_subtract_fusion.1
  165.1 4.3 %convolution_multiply_fusion.2 = f32[16,1024]{1,0:T(8,128)S(1)} fusion(f32[16,1024]{1,0:T(8,128)S(1)} %multiply_subtract_fusion.1, f32[1024,1024]{1,0:T(8,128)} %copy-done.3, f32[]{:T(128)} %bitcast), kind=kOutput, calls=%fused_computation.26 | convolution fusion | flops 201342976 | bytes 4325380 | tf_op jit(solution)/shard_map/dot_general | solution.py:42
  169.4 0.4 fusion.46
  169.8 1.9 collective-permute-start.5
  171.7 2.4 collective-permute-start.4
  174.1 0.2 fusion.23
  174.3 17.1 %all_gather.36 = f32[16,2048]{1,0:T(8,128)S(1)} all-gather(f32[16,128]{1,0:T(8,128)S(1)} %fusion.46), channel_id=1, replica_groups=mesh['grp'=2,'leaf'=16] {'leaf'}, dimensions={1}, use_global_device_ids=true | all-gather | bytes 139264 | tf_op jit(solution)/shard_map/all_gather | solution.py:85
  191.4 0.9 fusion.47
  192.3 17.8 %all-gather.3 = f32[256,128]{1,0:T(8,128)S(1)} all-gather(f32[16,128]{1,0:T(8,128)S(1)} %fusion.23), channel_id=5, replica_groups=mesh['grp'=2,'leaf'=16] {'leaf'}, dimensions={0}, use_global_device_ids=true | all-gather | bytes 139264 | tf_op jit(solution)/shard_map/all_gather | solution.py:86
  210.2 4.5 %all_gather.39 = f32[16,256]{1,0:T(8,128)S(1)} all-gather(f32[16,128]{1,0:T(8,128)S(1)} %reduce_sum.148), channel_id=1, replica_groups=mesh['grp'=2,'leaf'=16] {'grp'}, dimensions={1}, use_global_device_ids=true | all-gather | bytes 24576 | tf_op jit(solution)/shard_map/all_gather | solution.py:87
  214.7 0.2 fusion.48
  214.8 0.2 convolution_add_fusion.2
  215.1 0.0 collective-permute-done.5
  215.1 4.3 %fusion.45 = f32[16,1024]{1,0:T(8,128)S(1)} fusion(f32[16,1024]{1,0:T(8,128)S(1)} %collective-permute-done.5, f32[1024,1024]{1,0:T(8,128)} %get-tuple-element.49), kind=kOutput, calls=%fused_computation.82 | convolution fusion | flops 201326592 | bytes 4325376 | tf_op jit(solution)/shard_map/dot_general | solution.py:42
  219.4 2.1 fusion.18
  221.5 0.6 multiply_reduce_fusion.6
  222.1 43.0 %all-reduce = (f32[16]{0:T(128)S(1)}, f32[16]{0:T(128)S(1)}) all-reduce(f32[16]{0:T(128)S(1)} %get-tuple-element.31, f32[16]{0:T(128)S(1)} %get-tuple-element.30), channel_id=1, replica_groups=mesh['grp'=2,'leaf'=16] {'grp','leaf'}, use_global_device_ids=true, to_apply=%region_19.0 | all-reduce | flops 32 | bytes 256 | tf_op jit(solution)/shard_map/psum | solution.py:46
  265.2 0.7 multiply_subtract_fusion
  (19 shorter events, 0.1 us)
Async XLA Ops:
  0.6 17.1 %copy-start = (f32[1024,128]{1,0:T(8,128)S(1)}, f32[1024,128]{1,0:T(8,128)}, u32[]{:S(2)}) copy-start(f32[1024,128]{1,0:T(8,128)} %param.15) | copy-start | bytes 1572868
  0.6 89.0 %copy-start.6 = (f32[8,1024]{1,0:T(8,128)S(1)}, f32[8,1024]{1,0:T(8,128)}, u32[]{:S(2)}) copy-start(f32[8,1024]{1,0:T(8,128)} %param.13) | copy-start | bytes 98308
  0.7 88.8 %copy-start.8 = (f32[8]{0:T(128)S(1)}, f32[8]{0:T(128)}, u32[]{:S(2)}) copy-start(f32[8]{0:T(128)} %param.18) | copy-start | bytes 100
  0.7 105.1 %collective-permute-start.2 = (f32[8,1024]{1,0:T(8,128)}, f32[8,1024]{1,0:T(8,128)S(1)}, u32[]{:S(2)}, u32[]{:S(2)}) collective-permute-start(f32[8,1024]{1,0:T(8,128)} %param.13), channel_id=1, source_target_pairs={{1,0},{2,1},{3,2},{4,3},{5,4},{6,5},{7,6},{8,7},{9,8},{10,9},{11,1... | collective-permute-start | bytes 98312 | tf_op jit(solution)/shard_map/ppermute | solution.py:17
  3.6 99.6 %collective-permute-start = (f32[8,1024]{1,0:T(8,128)}, f32[8,1024]{1,0:T(8,128)S(1)}, u32[]{:S(2)}, u32[]{:S(2)}) collective-permute-start(f32[8,1024]{1,0:T(8,128)} %param.13), channel_id=1, source_target_pairs={{0,1},{1,2},{2,3},{3,4},{4,5},{5,6},{6,7},{7,8},{8,9},{9,10},{10,1... | collective-permute-start | bytes 98312 | tf_op jit(solution)/shard_map/ppermute | solution.py:16
  5.5 102.7 %collective-permute-start.3 = (f32[16,1024]{1,0:T(8,128)}, f32[16,1024]{1,0:T(8,128)S(1)}, u32[]{:S(2)}, u32[]{:S(2)}) collective-permute-start(f32[16,1024]{1,0:T(8,128)} %param.14), channel_id=1, source_target_pairs={{1,0},{2,1},{3,2},{4,3},{5,4},{6,5},{7,6},{8,7},{9,8},{10,9},{11,1... | collective-permute-start | bytes 196616 | tf_op jit(solution)/shard_map/ppermute | solution.py:17
  10.0 102.8 %collective-permute-start.1 = (f32[16,1024]{1,0:T(8,128)}, f32[16,1024]{1,0:T(8,128)S(1)}, u32[]{:S(2)}, u32[]{:S(2)}) collective-permute-start(f32[16,1024]{1,0:T(8,128)} %param.14), channel_id=1, source_target_pairs={{0,1},{1,2},{2,3},{3,4},{4,5},{5,6},{6,7},{7,8},{8,9},{9,10},{10,1... | collective-permute-start | bytes 196616 | tf_op jit(solution)/shard_map/ppermute | solution.py:16
  95.7 5.7 %copy-start.3 = (f32[1024,1024]{1,0:T(8,128)}, f32[1024,1024]{1,0:T(8,128)S(1)}, u32[]{:S(2)}) copy-start(f32[1024,1024]{1,0:T(8,128)S(1)} %exponential_multiply_fusion.2) | copy-start | bytes 12582916
  95.7 3.1 %copy-start.5 = (f32[1,128,128]{2,1,0:T(8,128)S(1)}, f32[1,128,128]{2,1,0:T(8,128)}, u32[]{:S(2)}) copy-start(f32[1,128,128]{2,1,0:T(8,128)} %param.16) | copy-start | bytes 196612
  95.7 3.3 %copy-start.4 = (f32[16,1024]{1,0:T(8,128)S(1)}, f32[16,1024]{1,0:T(8,128)}, u32[]{:S(2)}) copy-start(f32[16,1024]{1,0:T(8,128)} %param.14) | copy-start | bytes 196612
  108.2 4.6 %copy-start.7 = (f32[1024]{0:T(1024)S(1)}, f32[1024]{0:T(1024)}, u32[]{:S(2)}) copy-start(f32[1024]{0:T(1024)} %param.17) | copy-start | bytes 12292
  108.2 4.6 %copy-start.1 = (f32[1024,1024]{1,0:T(8,128)S(1)}, f32[1024,1024]{1,0:T(8,128)}, u32[]{:S(2)}) copy-start(f32[1024,1024]{1,0:T(8,128)} %get-tuple-element.48) | copy-start | bytes 12582916
  169.8 45.3 %collective-permute-start.5 = (f32[16,1024]{1,0:T(8,128)S(1)}, f32[16,1024]{1,0:T(8,128)S(1)}, u32[]{:S(2)}, u32[]{:S(2)}) collective-permute-start(f32[16,1024]{1,0:T(8,128)S(1)} %multiply_subtract_fusion.1), channel_id=1, source_target_pairs={{1,0},{2,1},{3,2},{4,3},{5,4},{6,5},{7,6},{8,7},{9,8},{10,9},{11,1... | collective-permute-start | bytes 196616 | tf_op jit(solution)/shard_map/ppermute | solution.py:17
  171.7 47.7 %collective-permute-start.4 = (f32[16,1024]{1,0:T(8,128)S(1)}, f32[16,1024]{1,0:T(8,128)S(1)}, u32[]{:S(2)}, u32[]{:S(2)}) collective-permute-start(f32[16,1024]{1,0:T(8,128)S(1)} %multiply_subtract_fusion.1), channel_id=1, source_target_pairs={{0,1},{1,2},{2,3},{3,4},{4,5},{5,6},{6,7},{7,8},{8,9},{9,10},{10,1... | collective-permute-start | bytes 196616 | tf_op jit(solution)/shard_map/ppermute | solution.py:16
  210.2 9.2 %copy-start.2 = (f32[1024,1024]{1,0:T(8,128)S(1)}, f32[1024,1024]{1,0:T(8,128)}, u32[]{:S(2)}) copy-start(f32[1024,1024]{1,0:T(8,128)} %get-tuple-element.48) | copy-start | bytes 12582916
